TPU v7x, 128 devices: a whole 4x4x4 slice. The times are simulated.
128 devices in a mesh: seq: 8 (over x, core), tensor: 4 (over z), bucket: 4 (over y).
Axes of the slice: x: 4, y: 4, z: 4, core: 2. Of those that a mesh axis runs over, the one named last changes fastest.
Arguments:
- queries: bfloat16 [4, 4096, 3072], P('bucket', ('seq', 'tensor')), may hold values from -6 to 6
- keys: bfloat16 [4, 4096, 3072], P('bucket', ('seq', 'tensor')), may hold values from -6 to 6
- values: bfloat16 [4, 4096, 3072], P('bucket', ('seq', 'tensor')), may hold values from -6 to 6
- lengths: int32 [4], P('bucket'), may hold values from 1024 to 4096, as said below
- out_weight: bfloat16 [3072, 3072], P(('seq', 'bucket'), 'tensor'), may hold values from -0.109375 to 0.109375
Outputs:
- projected: bfloat16 [4, 4096, 3072], P('bucket', ('seq', 'tensor'))
Inputs may be any that keep to these rules, and one draw needn't show every extreme that they name: `lengths`: each bucket has 1024 to 4096 live tokens, and at least one bucket has all 4096.
All inputs are finite; a program needn't handle non-finite values.
Results may differ from a plain program's by a relative error of at most 0.018.
Values may be sent and summed in bfloat16 or wider, within the bound.
A program may use at most 128 MiB of HBM per device.

v0:
```python
import jax
import jax.numpy as jnp
from jax import lax
from jax.sharding import PartitionSpec as P

HS = 128


MASKED_SCORE = -1e30


def in_one_piece(arrays, axis, dim, along):
    ends, at = ([], 0)
    for a in arrays[:-1]:
        at += a.shape[along]
        ends.append(at)
    both = jnp.concatenate(arrays, axis=along)
    return tuple(jnp.split(lax.all_gather(both, axis, axis=dim, tiled=True), ends, axis=along))


def in_order(blocks, dim):
    blocks = jnp.moveaxis(blocks, 0, dim)
    dims = blocks.shape
    return blocks.reshape(*dims[:dim], dims[dim] * dims[dim + 1], *dims[dim + 2 :])


def from_everyone(array, axis):
    devices = lax.axis_size(axis)
    return lax.all_to_all(
        jnp.broadcast_to(array[None], (devices, *array.shape)), axis, 0, 0, tiled=True
    )


def gather_directly(array, axis, dim):
    return in_order(from_everyone(array, axis), dim)


def shards(queries, keys, values, lengths, out_weight):
    tok_rows = queries.shape[1]
    n_tensor = lax.axis_size("tensor")
    tensor_index = lax.axis_index("tensor")
    live_len = lengths[0]
    local_q, local_k, local_v = (
        lax.all_to_all(queries[0], "seq", split_axis=1, concat_axis=0, tiled=True),
        lax.all_to_all(keys[0], "seq", split_axis=1, concat_axis=0, tiled=True),
        lax.all_to_all(values[0], "seq", split_axis=1, concat_axis=0, tiled=True),
    )
    row_count, col_count = local_q.shape
    head_count = col_count // HS
    query_heads = local_q.reshape(row_count, head_count, HS)

    def spots(first_row, total_rows):
        index_row = first_row + jnp.arange(total_rows, dtype=jnp.int32)
        owner = index_row // row_count
        within = index_row % row_count
        return (within // tok_rows * n_tensor + owner) * tok_rows + within % tok_rows

    query_usable = spots(tensor_index * row_count, row_count) < live_len
    initial = (
        jnp.full((row_count, head_count), MASKED_SCORE, jnp.float32),
        jnp.zeros((row_count, head_count), jnp.float32),
        jnp.zeros((row_count, head_count, HS), jnp.float32),
    )
    carried = initial
    first_row = jnp.int32(0)
    key_rows, value_rows = in_one_piece((local_k, local_v), "tensor", 0, 1)
    for offset in range(key_rows.shape[0] // row_count):
        row_peak, row_sum, accumulated = carried
        key_tile = key_rows[offset * row_count : (offset + 1) * row_count].reshape(
            row_count, head_count, HS
        )
        value_tile = value_rows[offset * row_count : (offset + 1) * row_count].reshape(
            row_count, head_count, HS
        )
        key_usable = spots(first_row + offset * row_count, row_count) < live_len
        scores = jnp.einsum(
            "qhd,khd->qhk", query_heads, key_tile, preferred_element_type=jnp.float32
        ) * HS ** (-0.5)
        scores = jnp.where(key_usable[None, None, :], scores, MASKED_SCORE)
        peak_new = jnp.maximum(row_peak, jnp.max(scores, axis=-1))
        exponent = jnp.where(key_usable[None, None, :], jnp.exp(scores - peak_new[..., None]), 0.0)
        rescale = jnp.exp(row_peak - peak_new)
        accumulated = accumulated * rescale[..., None] + jnp.einsum(
            "qhk,khd->qhd",
            exponent.astype(jnp.bfloat16),
            value_tile,
            preferred_element_type=jnp.float32,
        )
        carried = (peak_new, row_sum * rescale + jnp.sum(exponent, axis=-1), accumulated)
    row_peak, row_sum, accumulated = carried
    attended = accumulated / row_sum[..., None]
    mixed = jnp.where(query_usable[:, None], attended.reshape(row_count, col_count), 0.0).astype(
        jnp.bfloat16
    )
    restored = lax.all_to_all(mixed, "seq", split_axis=0, concat_axis=1, tiled=True)
    wide_weight = gather_directly(out_weight, "tensor", 1)
    summed = jnp.dot(
        restored,
        lax.all_gather(wide_weight, ("seq", "bucket"), axis=0, tiled=True),
        preferred_element_type=jnp.float32,
    )
    return summed.astype(jnp.bfloat16)[None]


def solution(mesh):
    in_specs = (
        P("bucket", ("seq", "tensor"), None),
        P("bucket", ("seq", "tensor"), None),
        P("bucket", ("seq", "tensor"), None),
        P("bucket"),
        P(("seq", "bucket"), "tensor"),
    )
    out_specs = P("bucket", ("seq", "tensor"), None)
    return jax.shard_map(shards, mesh=mesh, in_specs=in_specs, out_specs=out_specs, check_vma=False)
```

profile of v0, /device:TPU:1, one launch (start us, length us, event | category | flops | bytes accessed | tf_op | source)
XLA Modules:
  0.0 215.1 jit_solution(11350155920060903799)
XLA Ops:
  6.5 2.4 %copy.30 = bf16[1,128,3072]{1,2,0:T(8,128)(2,1)} copy(bf16[1,128,3072]{2,1,0:T(8,128)(2,1)} %param.7) | data formatting | bytes 1572864 | tf_op args[2]
  8.9 5.8 %all-to-all-start.1 = ((bf16[128,8,384]{0,2,1:T(8,128)(2,1)}), bf16[128,8,384]{0,2,1:T(8,128)(2,1)S(1)}, u32[]{:S(2)}, u32[]{:S(2)}) async-start(bf16[128,8,384]{0,2,1:T(8,128)(2,1)} %bitcast.3), calls=%async_computation.1 | async-start | bytes 1572864 | tf_op jit(solution)/shard_map/all_to_all | solution.py:46
  14.7 2.3 %copy.28 = bf16[1,128,3072]{1,2,0:T(8,128)(2,1)} copy(bf16[1,128,3072]{2,1,0:T(8,128)(2,1)} %param.6) | data formatting | bytes 1572864 | tf_op args[1]
  17.0 9.9 %all-to-all-done.1 = bf16[128,8,384]{0,2,1:T(8,128)(2,1)S(1)} async-done(((bf16[128,8,384]{0,2,1:T(8,128)(2,1)}), bf16[128,8,384]{0,2,1:T(8,128)(2,1)S(1)}, u32[]{:S(2)}, u32[]{:S(2)}) %all-to-all-start.1) | async-done | bytes 786464 | tf_op jit(solution)/shard_map/all_to_all | solution.py:46
  26.9 4.4 %all-to-all-start = ((bf16[128,8,384]{0,2,1:T(8,128)(2,1)}), bf16[128,8,384]{0,2,1:T(8,128)(2,1)S(1)}, u32[]{:S(2)}, u32[]{:S(2)}) async-start(bf16[128,8,384]{0,2,1:T(8,128)(2,1)} %bitcast.1), calls=%async_computation | async-start | bytes 1572864 | tf_op jit(solution)/shard_map/all_to_all | solution.py:45
  31.3 0.0 all-gather.3.cloned.1.call-start
  31.3 0.1 copy_bitcast_fusion
  31.4 12.1 %all-to-all-done = bf16[128,8,384]{0,2,1:T(8,128)(2,1)S(1)} async-done(((bf16[128,8,384]{0,2,1:T(8,128)(2,1)}), bf16[128,8,384]{0,2,1:T(8,128)(2,1)S(1)}, u32[]{:S(2)}, u32[]{:S(2)}) %all-to-all-start) | async-done | bytes 786464 | tf_op jit(solution)/shard_map/all_to_all | solution.py:45
  43.5 0.1 copy_bitcast_fusion.1
  43.6 1.3 pad_maximum_fusion
  44.9 0.0 all-gather.3.cloned.1.call-update
  45.0 0.0 all-gather.5.cloned.1.call-start
  45.0 0.0 copy-done.6
  45.1 13.8 %all_to_all.75 = bf16[4,96,768]{2,1,0:T(8,128)(2,1)S(1)} all-to-all(bf16[4,96,768]{2,1,0:T(8,128)(2,1)S(1)} %broadcast_in_dim.116), channel_id=1, replica_groups=mesh['seq'=8,'tensor'=4,'bucket'=4] {'tensor'}, dimensions={0} | all-to-all | bytes 1179648 | tf_op jit(solution)/shard_map/all_to_all | solution.py:29
  58.8 0.9 copy.62
  59.7 0.0 all-gather.5.cloned.1.call-update
  59.7 0.0 copy-done.5
  59.8 1.2 copy.32
  60.9 5.7 %all-to-all-start.2 = ((bf16[128,8,384]{0,2,1:T(8,128)(2,1)}), bf16[128,8,384]{0,2,1:T(8,128)(2,1)S(1)}, u32[]{:S(2)}, u32[]{:S(2)}) async-start(bf16[128,8,384]{0,2,1:T(8,128)(2,1)} %bitcast.6), calls=%async_computation.2 | async-start | bytes 1572864 | tf_op jit(solution)/shard_map/all_to_all | solution.py:44
  67.3 11.5 %all-to-all-done.2 = bf16[128,8,384]{0,2,1:T(8,128)(2,1)S(1)} async-done(((bf16[128,8,384]{0,2,1:T(8,128)(2,1)}), bf16[128,8,384]{0,2,1:T(8,128)(2,1)S(1)}, u32[]{:S(2)}, u32[]{:S(2)}) %all-to-all-start.2) | async-done | bytes 786464 | tf_op jit(solution)/shard_map/all_to_all | solution.py:44
  78.8 0.5 copy.33
  79.3 0.3 reshape.428
  79.6 32.0 %all-gather.3.cloned.1.call-done = bf16[4096,768]{0,1:T(8,128)(2,1)} async-done(((bf16[1024,768]{0,1:T(8,128)(2,1)}), bf16[4096,768]{0,1:T(8,128)(2,1)}) %all-gather.3.cloned.1.call-update) | async-done | bytes 6291472 | tf_op jit(solution)/shard_map/all_gather | solution.py:18
  111.6 4.9 %fusion.128 = (bf16[1024,384]{0,1:T(8,128)(2,1)}, bf16[1024,384]{0,1:T(8,128)(2,1)}, bf16[1024,384]{0,1:T(8,128)(2,1)S(1)}, bf16[1024,384]{0,1:T(8,128)(2,1)}, b...) fusion(bf16[4096,768]{0,1:T(8,128)(2,1)} %all-gather.3.cloned.1, ...), kind=kLoop, calls=%fused_computation.209 | loop fusion | bytes 12582912 | tf_op jit(solution)/shard_map/slice | solution.py:72
  116.5 2.5 %bitcast_reduce_fusion.3 = (f32[1024,3]{0,1:T(4,128)S(1)}, f32[3,1024,1024]{2,1,0:T(8,128)S(1)}) fusion(pred[1024]{0:T(1024)(128)(4,1)S(1)} %get-tuple-element.30, bf16[1024,3,128]{0,2,1:T(8,128)(2,1)S(1)} %bitcast.132, bf16[1024,3,128]{0,2,1:T(8,128)(2,1)S(1)} %reshape.428), kind=kOutput, calls=%fused_computation.13 | convolution fusion | flops 814740480 | bytes 14169088 | tf_op jit(solution)/shard_map/qhd,khd->qhk/dot_general | solution.py:76
  119.1 2.5 %bitcast_reduce_fusion = (f32[1024,3]{0,1:T(4,128)S(1)}, f32[3,1024,1024]{2,1,0:T(8,128)S(1)}) fusion(pred[1024]{0:T(1024)(128)(4,1)S(1)} %get-tuple-element.33, bf16[1024,3,128]{0,2,1:T(8,128)(2,1)S(1)} %bitcast.131, bf16[1024,3,128]{0,2,1:T(8,128)(2,1)S(1)} %reshape.428), kind=kOutput, calls=%fused_computation.1 | convolution fusion | flops 814740480 | bytes 14169088 | tf_op jit(solution)/shard_map/qhd,khd->qhk/dot_general | solution.py:76
  121.6 3.7 %bitcast_reduce_fusion.1 = (f32[1024,3]{0,1:T(4,128)S(1)}, f32[3,1024,1024]{2,1,0:T(8,128)S(1)}) fusion(pred[1024]{0:T(1024)(128)(4,1)S(1)} %get-tuple-element.32, bf16[1024,3,128]{0,2,1:T(8,128)(2,1)} %bitcast.130, bf16[1024,3,128]{0,2,1:T(8,128)(2,1)S(1)} %reshape.428), kind=kOutput, calls=%fused_computation.5 | convolution fusion | flops 814740480 | bytes 14169088 | tf_op jit(solution)/shard_map/qhd,khd->qhk/dot_general | solution.py:76
  125.4 0.0 copy-start
  125.4 6.3 %bitcast_reduce_fusion.2 = (f32[1024,3]{0,1:T(4,128)S(1)}, f32[3,1024,1024]{2,1,0:T(8,128)}) fusion(pred[1024]{0:T(1024)(128)(4,1)S(1)} %get-tuple-element.31, bf16[1024,3,128]{0,2,1:T(8,128)(2,1)S(1)} %bitcast.129, bf16[1024,3,128]{0,2,1:T(8,128)(2,1)S(1)} %reshape.428), kind=kOutput, calls=%fused_computation.9 | convolution fusion | flops 814740480 | bytes 14169088 | tf_op jit(solution)/shard_map/qhd,khd->qhk/dot_general | solution.py:76
  131.7 9.0 %fusion.10 = f32[1024,3]{0,1:T(4,128)S(1)} fusion(f32[3,1024,1024]{2,1,0:T(8,128)} %get-tuple-element.27, f32[1024,3]{0,1:T(4,128)S(1)} %get-tuple-element.11, pred[1024]{0:T(1024)(128)(4,1)S(1)} %get-tuple-element.31), kind=kLoop, calls=%fused_computation.22 | loop fusion | flops 15725568 | bytes 12608512 | tf_op jit(solution)/shard_map/reduce_sum | solution.py:89
  140.8 0.0 copy-done
  140.8 4.1 %fusion.12 = f32[1024,3]{0,1:T(4,128)S(1)} fusion(f32[3,1024,1024]{2,1,0:T(8,128)S(1)} %get-tuple-element.25, f32[1024,3]{0,1:T(4,128)S(1)} %get-tuple-element.10, pred[1024]{0:T(1024)(128)(4,1)S(1)} %get-tuple-element.32), kind=kLoop, calls=%fused_computation.24 | loop fusion | flops 15725568 | bytes 12608512 | tf_op jit(solution)/shard_map/reduce_sum | solution.py:89
  144.9 0.0 copy-start.4
  144.9 4.0 %fusion.14 = f32[1024,3]{0,1:T(4,128)S(1)} fusion(f32[3,1024,1024]{2,1,0:T(8,128)S(1)} %get-tuple-element.23, f32[1024,3]{0,1:T(4,128)S(1)} %get-tuple-element.9, pred[1024]{0:T(1024)(128)(4,1)S(1)} %get-tuple-element.33), kind=kLoop, calls=%fused_computation.26 | loop fusion | flops 15725568 | bytes 12608512 | tf_op jit(solution)/shard_map/reduce_sum | solution.py:89
  148.9 4.0 %fusion.8 = f32[1024,3]{0,1:T(4,128)S(1)} fusion(f32[3,1024,1024]{2,1,0:T(8,128)S(1)} %get-tuple-element.29, f32[1024,3]{0,1:T(4,128)S(1)} %get-tuple-element.21, pred[1024]{0:T(1024)(128)(4,1)S(1)} %get-tuple-element.30), kind=kLoop, calls=%fused_computation.20 | loop fusion | flops 15725568 | bytes 12608512 | tf_op jit(solution)/shard_map/reduce_sum | solution.py:89
  152.9 0.0 copy-start.3
  152.9 0.0 copy-done.4
  152.9 7.9 %fusion.20 = f32[3,128,1024]{2,1,0:T(8,128)} fusion(bf16[1024,3,128]{0,2,1:T(8,128)(2,1)S(1)} %bitcast.141, f32[3,1024,1024]{2,1,0:T(8,128)} %get-tuple-element.27, f32[1024,3]{0,1:T(4,128)S(1)} %get-tuple-element.11, pred[1024]{0:T(1024)(128)(4,1)S(1)} %get-tuple-element.31), kind=kOutput, calls=%fused_computation.30 | convolution fusion | flops 821035008 | bytes 14955520 | tf_op jit(solution)/shard_map/qhk,khd->qhd/dot_general | solution.py:83
  160.9 0.0 copy-done.3
  160.9 8.3 %fusion.18 = f32[3,128,1024]{2,1,0:T(8,128)} fusion(bf16[1024,3,128]{0,2,1:T(8,128)(2,1)S(1)} %bitcast.140, f32[3,1024,1024]{2,1,0:T(8,128)} %copy-done, f32[1024,3]{0,1:T(4,128)S(1)} %get-tuple-element.10, pred[1024]{0:T(1024)(128)(4,1)S(1)} %get-tuple-element.32), kind=kOutput, calls=%fused_computation.29 | convolution fusion | flops 821035008 | bytes 14955520 | tf_op jit(solution)/shard_map/qhk,khd->qhd/dot_general | solution.py:83
  169.2 0.0 copy-done.2
  169.2 4.4 %fusion.16 = f32[3,128,1024]{2,1,0:T(8,128)} fusion(bf16[1024,3,128]{0,2,1:T(8,128)(2,1)S(1)} %bitcast.139, f32[3,1024,1024]{2,1,0:T(8,128)S(1)} %get-tuple-element.23, f32[1024,3]{0,1:T(4,128)S(1)} %get-tuple-element.9, pred[1024]{0:T(1024)(128)(4,1)S(1)} %get-tuple-element.33), kind=kOutput, calls=%fused_computation.28 | convolution fusion | flops 821035008 | bytes 14955520 | tf_op jit(solution)/shard_map/qhk,khd->qhd/dot_general | solution.py:83
  173.5 0.0 copy-done.1
  173.5 6.2 %fusion.33 = bf16[1024,3,128]{0,2,1:T(8,128)(2,1)S(1)} fusion(f32[3,128,1024]{2,1,0:T(8,128)} %fusion.16, f32[3,128,1024]{2,1,0:T(8,128)} %fusion.18, f32[3,128,1024]{2,1,0:T(8,128)} %fusion.20, bf16[1024,3,128]{0,2,1:T(8,128)(2,1)S(1)} %bitcast.138, f32[3,1024,1024]{2,1,0:T(8,128)S(1)} %get-tuple-element.29, f32[1024,3]{0,1:T(4,128)S(1)} %get-tuple-element.21, ...), kind=kOutput, calls=%fused_computation.44 | convolution fusion | flops 824573952 | bytes 18949120 | tf_op jit(solution)/shard_map/qhk,khd->qhd/dot_general | solution.py:83
  179.8 0.2 copy.63
  179.9 0.2 fusion.37
  180.1 18.3 %all_to_all.76 = bf16[8,128,384]{1,2,0:T(8,128)(2,1)S(1)} all-to-all(bf16[8,128,384]{1,2,0:T(8,128)(2,1)S(1)} %fusion.37), channel_id=1, replica_groups=mesh['seq'=8,'tensor'=4,'bucket'=4] {'seq'}, dimensions={0} | all-to-all | bytes 1572864 | tf_op jit(solution)/shard_map/all_to_all | solution.py:95
  198.4 9.9 %fusion.32 = bf16[1,128,3072]{2,1,0:T(8,128)(2,1)} fusion(bf16[128,3072]{0,1:T(8,128)(2,1)S(1)} %bitcast.133, bf16[3072,3072]{1,0:T(8,128)(2,1)} %all-gather.5.cloned.1.call-done), kind=kOutput, calls=%fused_computation.41 | convolution fusion | flops 2416312320 | bytes 20447232 | tf_op jit(solution)/shard_map/dot_general | solution.py:97
  (11 shorter events, 0.2 us)
Async XLA Ops:
  6.5 38.5 %copy-start.6 = (bf16[96,768]{1,0:T(8,128)(2,1)S(1)}, bf16[96,768]{1,0:T(8,128)(2,1)}, u32[]{:S(2)}) copy-start(bf16[96,768]{1,0:T(8,128)(2,1)} %param.9) | copy-start | bytes 442372
  6.5 53.2 %copy-start.5 = (bf16[1,128,3072]{2,1,0:T(8,128)(2,1)S(1)}, bf16[1,128,3072]{2,1,0:T(8,128)(2,1)}, u32[]{:S(2)}) copy-start(bf16[1,128,3072]{2,1,0:T(8,128)(2,1)} %param.5) | copy-start | bytes 2359300
  8.9 17.9 %all-to-all-start.1 = ((bf16[128,8,384]{0,2,1:T(8,128)(2,1)}), bf16[128,8,384]{0,2,1:T(8,128)(2,1)S(1)}, u32[]{:S(2)}, u32[]{:S(2)}) async-start(bf16[128,8,384]{0,2,1:T(8,128)(2,1)} %bitcast.3), calls=%async_computation.1 | async-start | bytes 1572864 | tf_op jit(solution)/shard_map/all_to_all | solution.py:46
  26.9 16.6 %all-to-all-start = ((bf16[128,8,384]{0,2,1:T(8,128)(2,1)}), bf16[128,8,384]{0,2,1:T(8,128)(2,1)S(1)}, u32[]{:S(2)}, u32[]{:S(2)}) async-start(bf16[128,8,384]{0,2,1:T(8,128)(2,1)} %bitcast.1), calls=%async_computation | async-start | bytes 1572864 | tf_op jit(solution)/shard_map/all_to_all | solution.py:45
  31.3 80.3 %all-gather.3.cloned.1.call-start = ((), (), s32[]{:S(2)}) async-start(), calls=%async_computation.5 | async-start | bytes 7864320 | tf_op jit(solution)/shard_map/all_gather | solution.py:18
  45.0 153.4 %all-gather.5.cloned.1.call-start = ((), (), s32[]{:S(2)}) async-start(), calls=%async_computation.6 | async-start | bytes 19464192 | tf_op jit(solution)/shard_map/all_gather | solution.py:99
  60.9 17.8 %all-to-all-start.2 = ((bf16[128,8,384]{0,2,1:T(8,128)(2,1)}), bf16[128,8,384]{0,2,1:T(8,128)(2,1)S(1)}, u32[]{:S(2)}, u32[]{:S(2)}) async-start(bf16[128,8,384]{0,2,1:T(8,128)(2,1)} %bitcast.6), calls=%async_computation.2 | async-start | bytes 1572864 | tf_op jit(solution)/shard_map/all_to_all | solution.py:44
  125.4 15.4 %copy-start = (f32[3,1024,1024]{2,1,0:T(8,128)}, f32[3,1024,1024]{2,1,0:T(8,128)S(1)}, u32[]{:S(2)}) copy-start(f32[3,1024,1024]{2,1,0:T(8,128)S(1)} %get-tuple-element.25) | copy-start | bytes 37748740
  144.9 8.0 %copy-start.4 = (bf16[1024,384]{0,1:T(8,128)(2,1)S(1)}, bf16[1024,384]{0,1:T(8,128)(2,1)}, u32[]{:S(2)}) copy-start(bf16[1024,384]{0,1:T(8,128)(2,1)} %get-tuple-element.17) | copy-start | bytes 2359300
  152.9 8.0 %copy-start.3 = (bf16[1024,384]{0,1:T(8,128)(2,1)S(1)}, bf16[1024,384]{0,1:T(8,128)(2,1)}, u32[]{:S(2)}) copy-start(bf16[1024,384]{0,1:T(8,128)(2,1)} %get-tuple-element.15) | copy-start | bytes 2359300
  160.9 8.3 %copy-start.2 = (bf16[1024,384]{0,1:T(8,128)(2,1)S(1)}, bf16[1024,384]{0,1:T(8,128)(2,1)}, u32[]{:S(2)}) copy-start(bf16[1024,384]{0,1:T(8,128)(2,1)} %get-tuple-element.13) | copy-start | bytes 2359300
  169.2 4.4 %copy-start.1 = (bf16[1024,384]{0,1:T(8,128)(2,1)S(1)}, bf16[1024,384]{0,1:T(8,128)(2,1)}, u32[]{:S(2)}) copy-start(bf16[1024,384]{0,1:T(8,128)(2,1)} %get-tuple-element.12) | copy-start | bytes 2359300
Sparse Core Ops, SparseCore 0:
  45.1 66.4 all-gather.2
  113.9 79.4 all-gather.4
where the time goes:
time: 216 us; the launch traced here: 215 us
  waiting for transfers between devices  65.4 us (30%)
  matrix products  51.8 us (24%)
  blocking collectives  32 us (15%)
  other arithmetic  22.7 us (11%)
  starting transfers between devices  15.9 us (7%)
  between operations  14.2 us (7%)
  local copies, waits for them, and re-layouts  13 us (6%)
    all_gather x1, waiting for transfers between devices, in_one_piece(): lax.all_gather(both, axis, axis=dim, tiled=True)  32 us
    dot_general x4, matrix products, shards(): jnp.einsum('qhk,khd->qhd', exponent.astype(jnp.bfloat16), value_tile, pre...  26.8 us
    reduce_sum x4, other arithmetic, shards(): jnp.sum(exponent, axis=-1)  21.1 us
    all_to_all x1, blocking collectives, shards(): lax.all_to_all(mixed, 'seq', split_axis=0, concat_axis=1, tiled=True)  18.3 us
    dot_general x4, matrix products, shards(): jnp.einsum('qhd,khd->qhk', query_heads, key_tile, preferred_element_type=...  15.1 us
    all_to_all x1, blocking collectives, from_everyone(): lax.all_to_all(jnp.broadcast_to(array[None], (devices, *array.shape)), ax...  13.8 us
    all_to_all x1, waiting for transfers between devices, shards(): lax.all_to_all(keys[0], 'seq', split_axis=1, concat_axis=0, tiled=True)  12.1 us
    all_to_all x1, waiting for transfers between devices, shards(): lax.all_to_all(queries[0], 'seq', split_axis=1, concat_axis=0, tiled=True)  11.5 us
  transfers between devices with their start and end apart: 5, of which 4 were waited for; matrix products, arithmetic and copies ran while one was open for 34% of the time, Pallas kernels for 0%

commit v1 on v0

v1 whole, which is shorter than its diff:
```python
import functools
import math

import jax
import jax.numpy as jnp
from jax import lax
from jax.experimental import pallas as pl
from jax.experimental.pallas import tpu as pltpu
from jax.sharding import PartitionSpec as P

HS = 128
T = 128
MESH = pl.DeviceIdType.MESH
LOG2E_SCALED = math.log2(math.e) / math.sqrt(HS)
DEAD = -1e30
STEPS = 12


def place(z):
    inner = jnp.where((z == 1) | (z == 2), 1, 0)
    return inner * 2 + z // 2


def attend_kernel(
    len_ref, q_hbm, k_hbm, v_hbm, att_hbm,
    qb, kvb, ob, peak, acc, bias,
    q_send, kv_send, mate_send, part_send, o_send,
    q_recv, kv_recv, mate_recv, part_recv, o_recv,
):
    s, z, y = lax.axis_index("seq"), lax.axis_index("tensor"), lax.axis_index("bucket")
    x, c = s // 2, s % 2
    p = z // 2
    mate_z = p * 2 + 1 - z % 2
    own_base = jnp.where((z == 1) | (z == 2), 2, 0)
    my_block = s * 4 + place(z)

    def push(j, dx, cross):
        xd = (x + dx) % 4
        pd, zd = (p, z) if cross == 0 else (1 - p, 3 - z)
        col = pl.multiple_of(((xd * 2 + pd) * 3 + j) * HS, HS)
        dev = (xd * 2 + c, zd, y)
        slot = dx * 2 + cross
        rows = pl.ds(pl.multiple_of(slot * T, T), T)
        cols = pl.ds(col, HS)
        moves = (
            (q_hbm.at[0, :, cols], qb.at[j, rows], q_send.at[j, slot], q_recv.at[j]),
            (k_hbm.at[0, :, cols], kvb.at[j, my_block, 0], kv_send.at[j, slot, 0], kv_recv.at[j, dx]),
            (v_hbm.at[0, :, cols], kvb.at[j, my_block, 1], kv_send.at[j, slot, 1], kv_recv.at[j, dx]),
        )
        return moves, dev

    def start(j, dx, cross, which):
        moves, dev = push(j, dx, cross)

        def far():
            for w in which:
                src, dst, ss, rs = moves[w]
                pltpu.make_async_remote_copy(src, dst, ss, rs, device_id=dev, device_id_type=MESH).start()

        def near():
            for w in which:
                src, dst, ss, rs = moves[w]
                pltpu.make_async_copy(src, dst, rs).start()

        if cross == 1:
            far()
        else:
            pl.when(dx == 0)(near)
            pl.when(dx != 0)(far)

    @pl.loop(0, 3)
    def _(j):
        @pl.loop(0, 4)
        def _(dx):
            for cross in range(2):
                start(j, dx, cross, (0,))

        @pl.loop(0, 4)
        def _(dx):
            for cross in range(2):
                start(j, dx, cross, (1, 2))

    for sp in range(8):
        lane = lax.broadcasted_iota(jnp.int32, (8, 512), 1)
        quarter = lane // T
        zz = jnp.where(quarter == 0, 0, jnp.where(quarter == 1, 3, quarter - 1))
        token = (sp * 4 + zz) * T + lane % T
        bias[sp] = jnp.where(token < len_ref[0], 0.0, DEAD).astype(jnp.float32)

    def chunk(n, core):
        j, dx = n // 4, n % 4
        return j, dx, ((x - dx + 4) % 4) * 2 + core

    def mate_copy(n):
        j, dx, sp = chunk(n, c)
        part = kvb.at[j, pl.ds(sp * 4 + own_base, 2)]
        return pltpu.make_async_remote_copy(part, part, mate_send.at[n], mate_recv.at[n], device_id=(s, mate_z, y), device_id_type=MESH)

    def part_copy(n):
        j, dx, sp = chunk(n, c)
        part = kvb.at[j, pl.ds(sp * 4, 4)]
        return pltpu.make_async_remote_copy(part, part, part_send.at[n], part_recv.at[n], device_id=(x * 2 + 1 - c, z, y), device_id_type=MESH)

    def relay_to_mate(n):
        j, dx, sp = chunk(n, c)
        part = kvb.at[j, pl.ds(sp * 4 + own_base, 2)]
        pltpu.make_async_copy(part, part, kv_recv.at[j, dx]).wait()
        mate_copy(n).start()

    def relay_to_partner(n):
        mate_copy(n).wait_recv()
        part_copy(n).start()

    def attend(j, sp):
        k = kvb[j, pl.ds(sp * 4, 4), 0].reshape(512, HS)
        v = kvb[j, pl.ds(sp * 4, 4), 1].reshape(512, HS)
        scores = lax.dot_general(qb[j], k, (((1,), (1,)), ((), ())), preferred_element_type=jnp.float32)
        scores = scores + bias[sp, 0:1, :]
        old = peak[...]
        new = jnp.maximum(old, jnp.max(scores, axis=1, keepdims=True))
        weights = jnp.exp2((scores - new) * LOG2E_SCALED)
        rescale = jnp.exp2((old - new) * LOG2E_SCALED)
        wide = jnp.concatenate([v, jnp.ones_like(v)], axis=1)
        acc[...] = acc[...] * rescale + jnp.dot(weights.astype(jnp.bfloat16), wide, preferred_element_type=jnp.float32)
        peak[...] = new

    def o_copies(j, dx, cross):
        xs = (x - dx + 4) % 4
        zs = z if cross == 0 else 3 - z
        slot = dx * 2 + cross
        src = ob.at[j, pl.ds(pl.multiple_of(slot * T, T), T)]
        dst = att_hbm.at[:, pl.ds(pl.multiple_of(((x * 2 + p) * 3 + j) * HS, HS), HS)]
        far = pltpu.make_async_remote_copy(src, dst, o_send.at[j, slot], o_recv.at[j], device_id=(xs * 2 + c, zs, y), device_id_type=MESH)
        near = pltpu.make_async_copy(src, dst, o_recv.at[j])
        return far, near

    relay_to_mate(0)
    relay_to_mate(1)
    relay_to_partner(0)

    @pl.loop(0, STEPS)
    def _(n):
        j, dx = n // 4, n % 4

        @pl.when(n + 2 < STEPS)
        def _():
            relay_to_mate(n + 2)

        @pl.when(n + 1 < STEPS)
        def _():
            relay_to_partner(n + 1)

        @pl.when(dx == 0)
        def _():
            pltpu.make_async_copy(qb.at[j], qb.at[j], q_recv.at[j]).wait()
            peak[...] = jnp.full(peak.shape, DEAD, jnp.float32)
            acc[...] = jnp.zeros_like(acc)

        part_copy(n).wait_recv()

        @pl.loop(0, 2)
        def _(half):
            core = lax.rem(c + half, 2)
            attend(j, ((x - dx + 4) % 4) * 2 + core)

        @pl.when(dx == 3)
        def _():
            ob[j] = (acc[:, :HS] / acc[:, HS:]).astype(jnp.bfloat16)

            @pl.loop(0, 4)
            def _(e):
                for cross in range(2):
                    far, near = o_copies(j, e, cross)
                    if cross == 1:
                        far.start()
                    else:
                        pl.when(e == 0)(lambda near=near: near.start())
                        pl.when(e != 0)(lambda far=far: far.start())

    @pl.loop(0, 3)
    def _(j):
        @pl.loop(0, 4)
        def _(dx):
            for cross in range(2):
                moves, dev = push(j, dx, cross)
                far, near = o_copies(j, dx, cross)

                def drain(moves=moves, dev=dev, far=far):
                    for src, dst, ss, rs in moves:
                        pltpu.make_async_remote_copy(src, dst, ss, rs, device_id=dev, device_id_type=MESH).wait_send()
                    far.wait_send()

                if cross == 1:
                    drain()
                else:
                    pl.when(dx != 0)(drain)
        whole = ob.at[j]
        pltpu.make_async_copy(whole, whole, o_recv.at[j]).wait()

    @pl.loop(0, STEPS)
    def _(n):
        mate_copy(n).wait_send()
        part_copy(n).wait_send()


def attend_all(lengths, queries, keys, values):
    anywhere = pl.BlockSpec(memory_space=pl.ANY)
    dma = pltpu.SemaphoreType.DMA
    return pl.pallas_call(
        attend_kernel,
        out_shape=jax.ShapeDtypeStruct((T, 24 * HS), jnp.bfloat16),
        in_specs=[pl.BlockSpec(memory_space=pltpu.SMEM), anywhere, anywhere, anywhere],
        out_specs=anywhere,
        scratch_shapes=[
            pltpu.VMEM((3, 8 * T, HS), jnp.bfloat16),
            pltpu.VMEM((3, 32, 2, T, HS), jnp.bfloat16),
            pltpu.VMEM((3, 8 * T, HS), jnp.bfloat16),
            pltpu.VMEM((8 * T, 1), jnp.float32),
            pltpu.VMEM((8 * T, 2 * HS), jnp.float32),
            pltpu.VMEM((8, 8, 512), jnp.float32),
            dma((3, 8)), dma((3, 8, 2)), dma((STEPS,)), dma((STEPS,)), dma((3, 8)),
            dma((3,)), dma((3, 4)), dma((STEPS,)), dma((STEPS,)), dma((3,)),
        ],
        compiler_params=pltpu.CompilerParams(vmem_limit_bytes=56 * 2**20, has_side_effects=True),
        cost_estimate=pl.CostEstimate(flops=13 * 10**9, bytes_accessed=20 * 2**20, transcendentals=0),
        name="attend",
    )(lengths, queries, keys, values)


def shards(queries, keys, values, lengths, out_weight):
    s, z = lax.axis_index("seq"), lax.axis_index("tensor")
    weight = lax.all_gather(out_weight, ("seq", "bucket"), axis=0, tiled=True)
    weight = lax.all_gather(weight, "tensor", axis=1, tiled=True)
    attended = attend_all(lengths, queries, keys, values)
    token = (s * 4 + z) * T + jnp.arange(T, dtype=jnp.int32)
    attended = jnp.where((token < lengths[0])[:, None], attended, jnp.bfloat16(0))
    out = jnp.dot(attended, weight, preferred_element_type=jnp.float32)
    return out.astype(jnp.bfloat16)[None]


def solution(mesh):
    tokens = P("bucket", ("seq", "tensor"), None)
    return jax.shard_map(
        shards,
        mesh=mesh,
        in_specs=(tokens, tokens, tokens, P("bucket"), P(("seq", "bucket"), "tensor")),
        out_specs=tokens,
        check_vma=False,
    )
```

time: 216 us -> 280 us (1.30)
  Pallas kernels: 0 us -> 104 us
  waiting for transfers between devices: 65.4 us -> 151 us
  matrix products: 51.8 us -> 10.2 us
  blocking collectives: 32 us -> 0 us
  other arithmetic: 22.7 us -> 0.01 us
  starting transfers between devices: 15.9 us -> 0.04 us
  local copies, waits for them, and re-layouts: 13 us -> 0 us
    all_gather x2, waiting for transfers between devices: 32 us -> 150 us  [the longest x1 97.6 us: shards(): weight = lax.all_gather(weight, 'tensor', axis=1, tiled=True)]
    pallas_call x0 -> x1, Pallas kernels: none -> 104 us  [attend_all(): pl.pallas_call(attend_kernel, out_shape=jax.ShapeDtypeStruct((T, 24 * HS)...]
    dot_general x9 -> x1, matrix products: 51.8 us -> 10.2 us  [shards(): out = jnp.dot(attended, weight, preferred_element_type=jnp.float32)]
    all_to_all x3 -> x0, waiting for transfers between devices: 33.4 us -> none  [the longest x1 12.1 us: shards(): lax.all_to_all(keys[0], 'seq', split_axis=1, concat_axis=0, tiled=True)]
    all_to_all x2 -> x0, blocking collectives: 32 us -> none  [the longest x1 18.3 us: shards(): lax.all_to_all(mixed, 'seq', split_axis=0, concat_axis=1, tiled=True)]
    reduce_sum x4 -> x0, other arithmetic: 21.1 us -> none  [shards(): jnp.sum(exponent, axis=-1)]
    all_to_all x3 -> x0, starting transfers between devices: 15.9 us -> none  [the longest x1 5.79 us: shards(): lax.all_to_all(values[0], 'seq', split_axis=1, concat_axis=0, tiled=True)]
    unnamed x18 -> x0, local copies, waits for them, and re-layouts: 6.01 us -> none
  transfers between devices with their start and end apart: 5 -> 2, of which waited for: 4 -> 2; matrix products, arithmetic and copies ran while one was open for 34% -> 0% of each run, Pallas kernels for 0% -> 37%
where the time goes in v1:
time: 280 us; the launch traced here: 279 us
  waiting for transfers between devices  151 us (54%)
  Pallas kernels  104 us (37%)
  between operations  14.1 us (5%)
  matrix products  10.2 us (4%)
    pallas_call x1, Pallas kernels, attend_all(): pl.pallas_call(attend_kernel, out_shape=jax.ShapeDtypeStruct((T, 24 * HS)...  104 us
    all_gather x1, waiting for transfers between devices, shards(): weight = lax.all_gather(weight, 'tensor', axis=1, tiled=True)  97.6 us
    all_gather x1, waiting for transfers between devices, shards(): weight = lax.all_gather(out_weight, ('seq', 'bucket'), axis=0, tiled=True)  52.4 us
    dot_general x1, matrix products, shards(): out = jnp.dot(attended, weight, preferred_element_type=jnp.float32)  10.2 us
  transfers between devices with their start and end apart: 2, of which 2 were waited for; matrix products, arithmetic and copies ran while one was open for 0% of the time, Pallas kernels for 37%

profile of v1, /device:TPU:1, one launch (start us, length us, event | category | flops | bytes accessed | tf_op | source)
XLA Modules:
  0.0 279.5 jit_solution(17259551863373367659)
XLA Ops:
  6.5 0.0 all-gather.3.cloned.1.call-start
  6.5 0.7 all-gather.3.cloned.1.call-update
  7.3 0.0 all-gather.5.cloned.1.call-start
  7.3 52.4 %all-gather.3.cloned.1.call-done = bf16[3072,768]{1,0:T(8,128)(2,1)} async-done(((bf16[96,768]{1,0:T(8,128)(2,1)}), bf16[3072,768]{1,0:T(8,128)(2,1)}) %all-gather.3.cloned.1.call-update) | async-done | bytes 4718608 | tf_op jit(solution)/shard_map/all_gather | solution.py:232
  59.7 0.0 all-gather.5.cloned.1.call-update
  60.4 104.4 %attend.1 = bf16[128,3072]{1,0:T(8,128)(2,1)} custom-call(s32[1]{0:T(128)} %copy.6.len_ref, bf16[1,128,3072]{2,1,0:T(8,128)(2,1)} %q_hbm.1, bf16[1,128,3072]{2,1,0:T(8,128)(2,1)} %k_hbm.1, bf16[1,128,3072]{2,1,0:T(8,128)(2,1)} %v_hbm.1), custom_call_target="tpu_custom_call" | custom-call | flops 12999999488 | bytes 20971520 | tf_op jit(solution)/shard_map/attend/pallas_call | solution.py:209
  164.9 97.6 %all-gather.5.cloned.1.call-done = bf16[3072,3072]{1,0:T(8,128)(2,1)} async-done(((bf16[3072,768]{1,0:T(8,128)(2,1)}), bf16[3072,3072]{1,0:T(8,128)(2,1)}) %all-gather.5.cloned.1.call-update) | async-done | bytes 18874384 | tf_op jit(solution)/shard_map/all_gather | solution.py:233
  262.4 10.2 %fusion = bf16[1,128,3072]{2,1,0:T(8,128)(2,1)} fusion(bf16[3072,3072]{1,0:T(8,128)(2,1)} %all-gather.5.cloned.1.call-done, bf16[128,3072]{1,0:T(8,128)(2,1)} %attend.1, pred[128]{0:T(512)(128)(4,1)S(1)} %add_compare_fusion), kind=kOutput, calls=%fused_computation.1 | convolution fusion | flops 2416705536 | bytes 20447360 | tf_op jit(solution)/shard_map/dot_general | solution.py:237
  (1 shorter events, 0.0 us)
Async XLA Ops:
  6.5 53.2 %all-gather.3.cloned.1.call-start = ((), (), s32[]{:S(2)}) async-start(), calls=%async_computation | async-start | bytes 4866048 | tf_op jit(solution)/shard_map/all_gather | solution.py:232
  7.3 255.2 %all-gather.5.cloned.1.call-start = ((), (), s32[]{:S(2)}) async-start(), calls=%async_computation.1 | async-start | bytes 23592960 | tf_op jit(solution)/shard_map/all_gather | solution.py:233
Sparse Core Ops, SparseCore 0:
  9.6 50.0 all-gather.2
  61.4 200.9 all-gather.4

commit v2 on v1

v2 whole, which is shorter than its diff:
```python
import functools
import math

import jax
import jax.numpy as jnp
from jax import lax
from jax.experimental import pallas as pl
from jax.experimental.pallas import tpu as pltpu
from jax.sharding import PartitionSpec as P

HS = 128
T = 128
D = 3072
MESH = pl.DeviceIdType.MESH
LOG2E_SCALED = math.log2(math.e) / math.sqrt(HS)
DEAD = -1e30
STEPS = 12
ROWS_AT_ONCE = 128
GROUPS = (
    (0, 256, "zxy"),
    (256, 256, "zxy"),
    (512, 128, "yzx"),
    (640, 128, "xyz"),
)


def place(z):
    inner = jnp.where((z == 1) | (z == 2), 1, 0)
    return inner * 2 + z // 2


def kernel(
    len_ref, q_hbm, k_hbm, v_hbm, w_hbm, out_hbm,
    qb, kvb, ob, peak, acc, bias, wb, ox, mine, theirs, landed, out_vm,
    q_send, kv_send, mate_send, own_send, part_send, o_send, w_send, sum_send,
    q_recv, kv_recv, mate_recv, part_recv, o_recv, w_recv, sum_recv, w_own, out_sem,
):
    s, z, y = lax.axis_index("seq"), lax.axis_index("tensor"), lax.axis_index("bucket")
    x, c = s // 2, s % 2
    p = z // 2
    mate_z = p * 2 + 1 - z % 2
    partner = (x * 2 + 1 - c, z, y)
    own_base = jnp.where((z == 1) | (z == 2), 2, 0)
    my_block = s * 4 + place(z)

    def remote(src, dst, ss, rs, dev):
        return pltpu.make_async_remote_copy(src, dst, ss, rs, device_id=dev, device_id_type=MESH)

    barrier = pltpu.get_barrier_semaphore()
    peers = [((x + dx) % 4 * 2 + c, zz, y) for dx in range(4) for zz in (z, 3 - z) if not (dx == 0 and zz is z)]
    peers += [((x + dx) % 4 * 2 + 1 - c, zz, y) for dx in range(4) for zz in (z, 3 - z)]
    peers += [(s, (z + d) % 4, y) for d in (1, 2, 3)] + [(s, z, (y + d) % 4) for d in (1, 2, 3)]
    for dev in peers:
        pl.semaphore_signal(barrier, inc=1, device_id=dev, device_id_type=MESH)
    pl.semaphore_wait(barrier, len(peers))

    def q_move(j, dx, cross):
        xd = (x + dx) % 4
        pd, zd = (p, z) if cross == 0 else (1 - p, 3 - z)
        cols = pl.ds(pl.multiple_of(((xd * 2 + pd) * 3 + j) * HS, HS), HS)
        slot = dx * 2 + cross
        rows = pl.ds(pl.multiple_of(slot * T, T), T)
        return (q_hbm.at[0, :, cols], qb.at[j, rows], q_send.at[j, slot], q_recv.at[j], (xd * 2 + c, zd, y))

    def kv_move(j, dx, cross, which):
        xd = (x + dx) % 4
        pd, zd = (p, z) if cross == 0 else (1 - p, 3 - z)
        cols = pl.ds(pl.multiple_of(((xd * 2 + pd) * 3 + j) * HS, HS), HS)
        src = (k_hbm, v_hbm)[which].at[0, :, cols]
        return (src, kvb.at[j, my_block, which], kv_send.at[j, dx * 2 + cross, which], kv_recv.at[j, dx], (xd * 2 + c, zd, y))

    def own_to_mate(j, which):
        cols = pl.ds(pl.multiple_of(((x * 2 + p) * 3 + j) * HS, HS), HS)
        src = (k_hbm, v_hbm)[which].at[0, :, cols]
        return remote(src, kvb.at[j, my_block, which], own_send.at[j, which], mate_recv.at[j * 4], (s, mate_z, y))

    def begin(move, dx, cross):
        def far():
            remote(*move).start()

        def near():
            pltpu.make_async_copy(move[0], move[1], move[3]).start()

        if cross == 1:
            far()
        elif isinstance(dx, int):
            (near if dx == 0 else far)()
        else:
            pl.when(dx == 0)(near)
            pl.when(dx != 0)(far)

    def begin_kv(j, dx):
        for cross in range(2):
            for which in range(2):
                begin(kv_move(j, dx, cross, which), dx, cross)

    def begin_q(j):
        @pl.loop(0, 4)
        def _(dx):
            for cross in range(2):
                begin(q_move(j, dx, cross), dx, cross)

    at = {"x": x, "y": y, "z": z}

    def shifted(axis, d):
        to = dict(at)
        to[axis] = (at[axis] + d + 4) % 4
        return to

    def device(to):
        return (to["x"] * 2 + c, to["z"], to["y"])

    def slab(g, have, to, half=None):
        first, count, _ = GROUPS[g]
        split = "z" if "x" not in have else "x"
        pick = lambda axis: (
            (pl.ds(half * 2, 2) if half is not None and axis == split else pl.ds(0, 4)) if axis in have else to[axis]
        )
        rows = pl.ds(0, 384) if "y" in have else pl.ds(pl.multiple_of(to["y"] * 96, 32), 96)
        return wb.at[pick("x"), pick("z"), rows, pl.ds(first, count)]

    def w_copy(g, stage, d, half=None):
        first, count, order = GROUPS[g]
        axis, have = order[stage], order[:stage]
        whose = at if half is None else shifted(axis, -d)
        region = slab(g, have, whose, half)
        src = w_hbm.at[:, pl.ds(first, count)] if stage == 0 else region
        index = stage * 3 + d - 1 if stage < 2 else 6 + (0 if d == 1 else 1) + (0 if half is None else 2)
        return remote(src, region, w_send.at[g, index], w_recv.at[g, index], device(shifted(axis, d)))

    def w_begin(g, stage):
        for d in (1, 3, 2) if stage < 2 else (1, 3):
            w_copy(g, stage, d).start()

    def w_arrived(g, stage):
        for d in (1, 3, 2) if stage < 2 else (1, 3):
            w_copy(g, stage, d).wait_recv()

    def w_pass_on(g):
        w_copy(g, 2, 1, 0).start()
        w_copy(g, 2, 3, 1).start()

    def w_complete(g):
        w_copy(g, 2, 1, 0).wait_recv()
        w_copy(g, 2, 3, 1).wait_recv()

    def w_drain(g):
        for stage in range(3):
            for d in (1, 3, 2) if stage < 2 else (1, 3):
                w_copy(g, stage, d).wait_send()
        w_copy(g, 2, 1, 0).wait_send()
        w_copy(g, 2, 3, 1).wait_send()

    w_mine = pltpu.make_async_copy(w_hbm, wb.at[x, z, pl.ds(pl.multiple_of(y * 96, 32), 96)], w_own)

    begin_kv(0, 0)
    for which in range(2):
        own_to_mate(0, which).start()
    w_mine.start()
    begin_kv(0, 1)
    for g in range(2):
        w_begin(g, 0)
    begin_q(0)
    begin_kv(0, 2)
    begin_kv(0, 3)
    for j in (1, 2):
        for which in range(2):
            own_to_mate(j, which).start()
    for g in range(2, len(GROUPS)):
        w_begin(g, 0)

    @pl.loop(1, 3)
    def _(j):
        @pl.loop(0, 4)
        def _(dx):
            begin_kv(j, dx)

        begin_q(j)

    for sp in range(8):
        lane = lax.broadcasted_iota(jnp.int32, (8, 512), 1)
        quarter = lane // T
        zz = jnp.where(quarter == 0, 0, jnp.where(quarter == 1, 3, quarter - 1))
        token = (sp * 4 + zz) * T + lane % T
        bias[sp] = jnp.where(token < len_ref[0], 0.0, DEAD).astype(jnp.float32)

    def chunk(n):
        j, dx = n // 4, n % 4
        return j, dx, ((x - dx + 4) % 4) * 2 + c

    def mate_copy(n):
        j, dx, sp = chunk(n)
        part = kvb.at[j, pl.ds(sp * 4 + own_base, 2)]
        return remote(part, part, mate_send.at[n], mate_recv.at[n], (s, mate_z, y))

    def cross_copy(n):
        j, dx, sp = chunk(n)
        part = kvb.at[j, sp * 4 + place(3 - z)]
        return remote(part, part, mate_send.at[n], mate_recv.at[n], (s, mate_z, y))

    def part_copy(n):
        j, dx, sp = chunk(n)
        part = kvb.at[j, pl.ds(sp * 4, 4)]
        return remote(part, part, part_send.at[n], part_recv.at[n], partner)

    def relay_to_mate(n):
        j, dx, sp = chunk(n)
        part = kvb.at[j, pl.ds(sp * 4 + own_base, 2)]
        pltpu.make_async_copy(part, part, kv_recv.at[j, dx]).wait()

        def all_of_it():
            mate_copy(n).start()

        def the_rest():
            cross_copy(n).start()

        if isinstance(dx, int):
            (the_rest if dx == 0 else all_of_it)()
        else:
            pl.when(dx == 0)(the_rest)
            pl.when(dx != 0)(all_of_it)

    def relay_to_partner(n):
        mate_copy(n).wait_recv()
        part_copy(n).start()

    def attend(j, dx):
        base = ((x - dx + 4) % 4) * 8
        k = kvb[j, pl.ds(base, 8), 0].reshape(1024, HS)
        v = kvb[j, pl.ds(base, 8), 1].reshape(1024, HS)
        wide = jnp.concatenate([v, jnp.ones_like(v)], axis=1)
        both = (x - dx + 4) % 4 * 2
        dead = jnp.concatenate([bias[both, 0:1, :], bias[both + 1, 0:1, :]], axis=1)
        for first in range(0, 8 * T, ROWS_AT_ONCE):
            r = pl.ds(first, ROWS_AT_ONCE)
            scores = lax.dot_general(qb[j, r], k, (((1,), (1,)), ((), ())), preferred_element_type=jnp.float32) + dead
            old = peak[r, :]
            new = jnp.maximum(old, jnp.max(scores, axis=1, keepdims=True))
            weights = jnp.exp2((scores - new) * LOG2E_SCALED).astype(jnp.bfloat16)
            rescale = jnp.exp2((old - new) * LOG2E_SCALED)
            acc[r, :] = acc[r, :] * rescale + jnp.dot(weights, wide, preferred_element_type=jnp.float32)
            peak[r, :] = new

    def o_move(j, dx, cross):
        xs = (x - dx + 4) % 4
        zs = z if cross == 0 else 3 - z
        slot = dx * 2 + cross
        src = ob.at[j, pl.ds(pl.multiple_of(slot * T, T), T)]
        dst = ox.at[pl.ds(pl.multiple_of(c * T, T), T), pl.ds(pl.multiple_of((x * 3 + j) * HS, HS), HS)]
        return src, dst, o_send.at[j, slot], o_recv.at[j], (xs * 2 + p, zs, y)

    def send_attended(j):
        @pl.loop(0, 4)
        def _(dx):
            for cross in range(2):
                move = o_move(j, dx, cross)

                def far(move=move):
                    remote(*move).start()

                def near(move=move):
                    pltpu.make_async_copy(move[0], move[1], move[3]).start()

                if cross == 1:
                    far()
                else:
                    pl.when((dx == 0) & (p == c))(near)
                    pl.when((dx != 0) | (p != c))(far)

    relay_to_mate(0)
    for g in range(2):
        w_arrived(g, 0)
    w_mine.wait()
    for g in range(2):
        w_begin(g, 1)
    relay_to_mate(1)
    relay_to_partner(0)

    events = {
        1: lambda: (w_arrived(0, 1), w_begin(0, 2), w_arrived(1, 1), w_begin(1, 2)),
        2: lambda: (w_arrived(2, 0), w_begin(2, 1), w_arrived(3, 0), w_begin(3, 1)),
        6: lambda: (w_arrived(2, 1), w_begin(2, 2), w_arrived(3, 1), w_begin(3, 2)),
        9: lambda: (w_arrived(0, 2), w_pass_on(0)),
    }

    @pl.loop(0, STEPS)
    def _(n):
        j, dx = n // 4, n % 4

        @pl.when(n + 2 < STEPS)
        def _():
            relay_to_mate(n + 2)

        @pl.when(n + 1 < STEPS)
        def _():
            relay_to_partner(n + 1)

        for when, event in events.items():
            pl.when(n == when)(lambda event=event: event() and None)

        @pl.when(dx == 0)
        def _():
            pltpu.make_async_copy(qb.at[j], qb.at[j], q_recv.at[j]).wait()
            peak[...] = jnp.full(peak.shape, DEAD, jnp.float32)
            acc[...] = jnp.zeros_like(acc)

        part_copy(n).wait_recv()
        attend(j, dx)

        @pl.when(dx == 3)
        def _():
            ob[j] = (acc[:, :HS] / acc[:, HS:]).astype(jnp.bfloat16)
            send_attended(j)

    w_arrived(2, 2)
    w_pass_on(2)
    w_arrived(3, 2)
    w_pass_on(3)
    w_arrived(1, 2)
    w_pass_on(1)

    for j in range(3):
        part = ob.at[j]
        pltpu.make_async_copy(part, part, o_recv.at[j]).wait()

    def sum_copy(g, zb):
        first, count, _ = GROUPS[g]
        cols = pl.ds(pl.multiple_of(zb * 768 + first, HS), count)
        return remote(theirs.at[:, cols], landed.at[:, cols], sum_send.at[g, zb], sum_recv.at[g, zb], partner)

    order = (2, 3, 0, 1)
    for g in order:
        w_complete(g)
        first, count, _ = GROUPS[g]

        @pl.loop(0, 4)
        def _(zb, first=first, count=count, g=g):
            cols = pl.ds(pl.multiple_of(zb * 768 + first, HS), count)
            total = jnp.zeros((2 * T, count), jnp.float32)
            for xb in range(4):
                total += jnp.dot(
                    ox[:, xb * 384 : (xb + 1) * 384], wb[xb, zb, :, first : first + count], preferred_element_type=jnp.float32
                )
            low, high = total[:T], total[T:]
            mine[:, cols] = jnp.where(c == 0, low, high)
            theirs[:, cols] = jnp.where(c == 0, high, low)
            sum_copy(g, zb).start()

    token = (s * 4 + z) * T + lax.broadcasted_iota(jnp.int32, (T, 1), 0)
    live = token < len_ref[0]
    for g in order:
        first, count, _ = GROUPS[g]

        @pl.loop(0, 4)
        def _(zb, first=first, count=count, g=g):
            cols = pl.ds(pl.multiple_of(zb * 768 + first, HS), count)
            sum_copy(g, zb).wait_recv()
            out_vm[:, cols] = jnp.where(live, mine[:, cols] + landed[:, cols], 0.0).astype(jnp.bfloat16)

    done = pltpu.make_async_copy(out_vm, out_hbm.at[0], out_sem)
    done.start()

    @pl.loop(0, 3)
    def _(j):
        for which in range(2):
            own_to_mate(j, which).wait_send()

        @pl.loop(0, 4)
        def _(dx):
            for cross in range(2):
                moves = [q_move(j, dx, cross), kv_move(j, dx, cross, 0), kv_move(j, dx, cross, 1)]
                o = o_move(j, dx, cross)

                def drain(moves=moves):
                    for move in moves:
                        remote(*move).wait_send()

                def drain_o(o=o):
                    remote(*o).wait_send()

                if cross == 1:
                    drain()
                    drain_o()
                else:
                    pl.when(dx != 0)(drain)
                    pl.when((dx != 0) | (p != c))(drain_o)

    @pl.loop(0, STEPS)
    def _(n):
        pl.when(n % 4 == 0)(lambda: cross_copy(n).wait_send())
        pl.when(n % 4 != 0)(lambda: mate_copy(n).wait_send())
        part_copy(n).wait_send()

    for g in range(len(GROUPS)):
        w_drain(g)

        @pl.loop(0, 4)
        def _(zb, g=g):
            sum_copy(g, zb).wait_send()

    done.wait()


def everything(lengths, queries, keys, values, weight):
    anywhere = pl.BlockSpec(memory_space=pl.ANY)
    dma = pltpu.SemaphoreType.DMA
    bf16, f32, vmem = jnp.bfloat16, jnp.float32, pltpu.VMEM
    groups = len(GROUPS)
    return pl.pallas_call(
        kernel,
        out_shape=jax.ShapeDtypeStruct((1, T, D), bf16),
        in_specs=[pl.BlockSpec(memory_space=pltpu.SMEM)] + [anywhere] * 4,
        out_specs=anywhere,
        scratch_shapes=[
            vmem((3, 8 * T, HS), bf16),
            vmem((3, 32, 2, T, HS), bf16),
            vmem((3, 8 * T, HS), bf16),
            vmem((8 * T, 1), f32),
            vmem((8 * T, 2 * HS), f32),
            vmem((8, 8, 512), f32),
            vmem((4, 4, 384, 768), bf16),
            vmem((2 * T, 1536), bf16),
            vmem((T, D), f32),
            vmem((T, D), f32),
            vmem((T, D), f32),
            vmem((T, D), bf16),
            dma((3, 8)), dma((3, 8, 2)), dma((STEPS,)), dma((3, 2)), dma((STEPS,)), dma((3, 8)), dma((groups, 10)), dma((groups, 4)),
            dma((3,)), dma((3, 4)), dma((STEPS,)), dma((STEPS,)), dma((3,)), dma((groups, 10)), dma((groups, 4)), dma(()), dma(()),
        ],
        compiler_params=pltpu.CompilerParams(vmem_limit_bytes=60 * 2**20, has_side_effects=True, collective_id=0),
        cost_estimate=pl.CostEstimate(flops=16 * 10**9, bytes_accessed=30 * 2**20, transcendentals=0),
        name="attend",
    )(lengths, queries, keys, values, weight)


def shards(queries, keys, values, lengths, out_weight):
    return everything(lengths, queries, keys, values, out_weight)


def solution(mesh):
    tokens = P("bucket", ("seq", "tensor"), None)
    return jax.shard_map(
        shards,
        mesh=mesh,
        in_specs=(tokens, tokens, tokens, P("bucket"), P(("seq", "bucket"), "tensor")),
        out_specs=tokens,
        check_vma=False,
    )
```

time: 280 us -> 134 us (0.48)
  waiting for transfers between devices: 151 us -> 0 us
  Pallas kernels: 104 us -> 131 us
  between operations: 14.1 us -> 0.66 us
  matrix products: 10.2 us -> 0 us
    all_gather x2 -> x0, waiting for transfers between devices: 150 us -> none  [the longest x1 97.6 us: shards(): weight = lax.all_gather(weight, 'tensor', axis=1, tiled=True)]
    pallas_call x1, Pallas kernels: 104 us -> 131 us  [everything(): pl.pallas_call(kernel, out_shape=jax.ShapeDtypeStruct((1, T, D), bf16), i...]
    dot_general x1 -> x0, matrix products: 10.2 us -> none  [shards(): out = jnp.dot(attended, weight, preferred_element_type=jnp.float32)]
  transfers between devices with their start and end apart: 2 -> 0, of which waited for: 2 -> 0; matrix products, arithmetic and copies ran while one was open for 0% -> 0% of each run, Pallas kernels for 37% -> 0%
where the time goes in v2:
time: 134 us; the launch traced here: 133 us
  Pallas kernels  131 us (98%)
  local copies, waits for them, and re-layouts  2.06 us (2%)
    pallas_call x1, Pallas kernels, everything(): pl.pallas_call(kernel, out_shape=jax.ShapeDtypeStruct((1, T, D), bf16), i...  131 us

profile of v2, /device:TPU:1, one launch (start us, length us, event | category | flops | bytes accessed | tf_op | source)
XLA Modules:
  0.0 133.4 jit_solution(17731028236831835515)
XLA Ops:
  0.7 130.7 %attend.1 = bf16[1,128,3072]{2,1,0:T(8,128)(2,1)} custom-call(s32[1]{0:T(128)S(6)} %copy.7.len_ref, bf16[1,128,3072]{2,1,0:T(8,128)(2,1)} %q_hbm.1, bf16[1,128,3072]{2,1,0:T(8,128)(2,1)} %k_hbm.1, bf16[1,128,3072]{2,1,0:T(8,128)(2,1)} %v_hbm.1, bf16[96,768]{1,0:T(8,128)(2,1)} %w_hbm.1), custom_call_target="tpu_custom_call" | custom-call | flops 16000000000 | bytes 31457280 | tf_op jit(solution)/shard_map/attend/pallas_call | solution.py:409
  131.4 2.1 %copy.8 = bf16[1,128,3072]{2,1,0:T(8,128)(2,1)} copy(bf16[1,128,3072]{2,1,0:T(8,128)(2,1)} %attend.1) | data formatting | bytes 1572864

commit v3 on v2

--- a/solution.py
+++ b/solution.py
@@ -16,9 +16,10 @@
 DEAD = -1e30
 STEPS = 12
 ROWS_AT_ONCE = 128
+RINGS = 2
 GROUPS = (
     (0, 256, "zxy"),
-    (256, 256, "zxy"),
+    (256, 256, "xzy"),
     (512, 128, "yzx"),
     (640, 128, "xyz"),
 )
@@ -33,7 +34,7 @@
     len_ref, q_hbm, k_hbm, v_hbm, w_hbm, out_hbm,
     qb, kvb, ob, peak, acc, bias, wb, ox, mine, theirs, landed, out_vm,
     q_send, kv_send, mate_send, own_send, part_send, o_send, w_send, sum_send,
-    q_recv, kv_recv, mate_recv, part_recv, o_recv, w_recv, sum_recv, w_own, out_sem,
+    q_recv, kv_recv, mate_recv, part_recv, o_recv, w_recv, r_recv, sum_recv, w_own, out_sem,
 ):
     s, z, y = lax.axis_index("seq"), lax.axis_index("tensor"), lax.axis_index("bucket")
     x, c = s // 2, s % 2
@@ -60,19 +61,19 @@
         cols = pl.ds(pl.multiple_of(((xd * 2 + pd) * 3 + j) * HS, HS), HS)
         slot = dx * 2 + cross
         rows = pl.ds(pl.multiple_of(slot * T, T), T)
-        return (q_hbm.at[0, :, cols], qb.at[j, rows], q_send.at[j, slot], q_recv.at[j], (xd * 2 + c, zd, y))
+        return (q_hbm.at[0, :, cols], qb.at[j, rows], q_send.at[j], q_recv.at[j], (xd * 2 + c, zd, y))
 
     def kv_move(j, dx, cross, which):
         xd = (x + dx) % 4
         pd, zd = (p, z) if cross == 0 else (1 - p, 3 - z)
         cols = pl.ds(pl.multiple_of(((xd * 2 + pd) * 3 + j) * HS, HS), HS)
         src = (k_hbm, v_hbm)[which].at[0, :, cols]
-        return (src, kvb.at[j, my_block, which], kv_send.at[j, dx * 2 + cross, which], kv_recv.at[j, dx], (xd * 2 + c, zd, y))
+        return (src, kvb.at[j, my_block, which], kv_send.at[j], kv_recv.at[j, dx], (xd * 2 + c, zd, y))
 
     def own_to_mate(j, which):
         cols = pl.ds(pl.multiple_of(((x * 2 + p) * 3 + j) * HS, HS), HS)
         src = (k_hbm, v_hbm)[which].at[0, :, cols]
-        return remote(src, kvb.at[j, my_block, which], own_send.at[j, which], mate_recv.at[j * 4], (s, mate_z, y))
+        return remote(src, kvb.at[j, my_block, which], own_send, mate_recv.at[j * 4], (s, mate_z, y))
 
     def begin(move, dx, cross):
         def far():
@@ -94,11 +95,17 @@
             for which in range(2):
                 begin(kv_move(j, dx, cross, which), dx, cross)
 
-    def begin_q(j):
-        @pl.loop(0, 4)
-        def _(dx):
-            for cross in range(2):
-                begin(q_move(j, dx, cross), dx, cross)
+    def begin_q(j, dx):
+        for cross in range(2):
+            begin(q_move(j, dx, cross), dx, cross)
+
+    def begin_chunk(m):
+        j, dx = m // 4, m % 4
+        begin_kv(j, dx)
+        if isinstance(m, int):
+            begin_q(j + 1, dx)
+        else:
+            pl.when(j < 2)(lambda: begin_q(j + 1, dx))
 
     at = {"x": x, "y": y, "z": z}
 
@@ -125,16 +132,26 @@
         whose = at if half is None else shifted(axis, -d)
         region = slab(g, have, whose, half)
         src = w_hbm.at[:, pl.ds(first, count)] if stage == 0 else region
-        index = stage * 3 + d - 1 if stage < 2 else 6 + (0 if d == 1 else 1) + (0 if half is None else 2)
-        return remote(src, region, w_send.at[g, index], w_recv.at[g, index], device(shifted(axis, d)))
-
-    def w_begin(g, stage):
-        for d in (1, 3, 2) if stage < 2 else (1, 3):
+        if stage == 0:
+            arrival = 0
+        elif stage == 1:
+            arrival = d
+        else:
+            arrival = 4 + (0 if d == 1 else 1) + (0 if half is None else 2)
+        return remote(src, region, w_send.at[g, stage + (0 if half is None else 1)], w_recv.at[g, arrival], device(shifted(axis, d)))
+
+    def w_begin(g, stage, ds=None):
+        for d in ds or ((1, 3, 2) if stage < 2 else (1, 3)):
             w_copy(g, stage, d).start()
 
     def w_arrived(g, stage):
-        for d in (1, 3, 2) if stage < 2 else (1, 3):
-            w_copy(g, stage, d).wait_recv()
+        if stage == 0:
+            first, count, _ = GROUPS[g]
+            three = wb.at[0, 0, pl.ds(0, 288), pl.ds(first, count)]
+            pltpu.make_async_copy(three, three, w_recv.at[g, 0]).wait()
+        else:
+            for d in (1, 3, 2) if stage < 2 else (1, 3):
+                w_copy(g, stage, d).wait_recv()
 
     def w_pass_on(g):
         w_copy(g, 2, 1, 0).start()
@@ -144,12 +161,49 @@
         w_copy(g, 2, 1, 0).wait_recv()
         w_copy(g, 2, 3, 1).wait_recv()
 
+    def settle(region, sem):
+        pltpu.make_async_copy(region, region, sem).wait()
+
     def w_drain(g):
-        for stage in range(3):
-            for d in (1, 3, 2) if stage < 2 else (1, 3):
-                w_copy(g, stage, d).wait_send()
-        w_copy(g, 2, 1, 0).wait_send()
-        w_copy(g, 2, 3, 1).wait_send()
+        first, count, _ = GROUPS[g]
+        settle(wb.at[0, 0, pl.ds(0, 288), pl.ds(0, count)], w_send.at[g, 0])
+        settle(wb.at[0, 0, pl.ds(0, 96 * count // 64), :], w_send.at[g, 1])
+        settle(wb.at[0, :, pl.ds(0, 256 if g < RINGS else 128), :], w_send.at[g, 2])
+        if g < RINGS:
+            settle(wb.at[0, :, pl.ds(0, 128), :], w_send.at[g, 3])
+        else:
+            settle(wb.at[0, 0, pl.ds(0, 256), :], w_send.at[g, 3])
+
+    def ring_copy(g, u, d, onward=False):
+        first, count, order = GROUPS[g]
+        whose = (y + 4 - d) % 4 if onward else y
+        part = pl.ds(0 if d == 1 else 2, 2) if onward else pl.ds(0, 4)
+        rows = pl.ds(pl.multiple_of(whose * 96, 32), 96)
+        if order[1] == "x":
+            region = wb.at[(x + 4 - u) % 4, part, rows, pl.ds(first, count)]
+        else:
+            region = wb.at[part, (z + 4 - u) % 4, rows, pl.ds(first, count)]
+        index = (2 if onward else 0) + (0 if d == 1 else 1)
+        return remote(region, region, w_send.at[g, 3 if onward else 2], r_recv.at[g, u, index], (s, z, (y + d) % 4))
+
+    def ring_begin(g, u):
+        for d in (1, 3):
+            ring_copy(g, u, d).start()
+
+    def ring_pass_on(g, u):
+        for d in (1, 3):
+            ring_copy(g, u, d).wait_recv()
+            ring_copy(g, u, d, True).start()
+
+    def ring_complete(g):
+        for u in range(4):
+            for d in (1, 3):
+                ring_copy(g, u, d, True).wait_recv()
+
+    def slab_arrived(g, *us):
+        for u in us:
+            w_copy(g, 1, u).wait_recv()
+            ring_begin(g, u)
 
     w_mine = pltpu.make_async_copy(w_hbm, wb.at[x, z, pl.ds(pl.multiple_of(y * 96, 32), 96)], w_own)
 
@@ -158,24 +212,12 @@
         own_to_mate(0, which).start()
     w_mine.start()
     begin_kv(0, 1)
-    for g in range(2):
+    for g in range(RINGS):
         w_begin(g, 0)
-    begin_q(0)
-    begin_kv(0, 2)
-    begin_kv(0, 3)
-    for j in (1, 2):
-        for which in range(2):
-            own_to_mate(j, which).start()
-    for g in range(2, len(GROUPS)):
-        w_begin(g, 0)
-
-    @pl.loop(1, 3)
-    def _(j):
-        @pl.loop(0, 4)
-        def _(dx):
-            begin_kv(j, dx)
-
-        begin_q(j)
+    for dx in range(4):
+        begin_q(0, dx)
+    begin_q(1, 0)
+    begin_q(1, 1)
 
     for sp in range(8):
         lane = lax.broadcasted_iota(jnp.int32, (8, 512), 1)
@@ -191,17 +233,17 @@
     def mate_copy(n):
         j, dx, sp = chunk(n)
         part = kvb.at[j, pl.ds(sp * 4 + own_base, 2)]
-        return remote(part, part, mate_send.at[n], mate_recv.at[n], (s, mate_z, y))
+        return remote(part, part, mate_send, mate_recv.at[n], (s, mate_z, y))
 
     def cross_copy(n):
         j, dx, sp = chunk(n)
         part = kvb.at[j, sp * 4 + place(3 - z)]
-        return remote(part, part, mate_send.at[n], mate_recv.at[n], (s, mate_z, y))
+        return remote(part, part, mate_send, mate_recv.at[n], (s, mate_z, y))
 
     def part_copy(n):
         j, dx, sp = chunk(n)
         part = kvb.at[j, pl.ds(sp * 4, 4)]
-        return remote(part, part, part_send.at[n], part_recv.at[n], partner)
+        return remote(part, part, part_send, part_recv.at[n], partner)
 
     def relay_to_mate(n):
         j, dx, sp = chunk(n)
@@ -246,8 +288,8 @@
         zs = z if cross == 0 else 3 - z
         slot = dx * 2 + cross
         src = ob.at[j, pl.ds(pl.multiple_of(slot * T, T), T)]
-        dst = ox.at[pl.ds(pl.multiple_of(c * T, T), T), pl.ds(pl.multiple_of((x * 3 + j) * HS, HS), HS)]
-        return src, dst, o_send.at[j, slot], o_recv.at[j], (xs * 2 + p, zs, y)
+        dst = ox.at[pl.ds(pl.multiple_of(jnp.where(p == c, 0, T), T), T), pl.ds(pl.multiple_of((x * 3 + j) * HS, HS), HS)]
+        return src, dst, o_send, o_recv.at[j], (xs * 2 + p, zs, y)
 
     def send_attended(j):
         @pl.loop(0, 4)
@@ -268,19 +310,31 @@
                     pl.when((dx != 0) | (p != c))(far)
 
     relay_to_mate(0)
-    for g in range(2):
+    begin_chunk(2)
+    relay_to_mate(1)
+    begin_chunk(3)
+    w_mine.wait()
+    for g in range(RINGS):
         w_arrived(g, 0)
-    w_mine.wait()
-    for g in range(2):
-        w_begin(g, 1)
-    relay_to_mate(1)
+        ring_begin(g, 0)
     relay_to_partner(0)
 
+    def own_heads():
+        for j in (1, 2):
+            for which in range(2):
+                own_to_mate(j, which).start()
+
     events = {
-        1: lambda: (w_arrived(0, 1), w_begin(0, 2), w_arrived(1, 1), w_begin(1, 2)),
-        2: lambda: (w_arrived(2, 0), w_begin(2, 1), w_arrived(3, 0), w_begin(3, 1)),
-        6: lambda: (w_arrived(2, 1), w_begin(2, 2), w_arrived(3, 1), w_begin(3, 2)),
-        9: lambda: (w_arrived(0, 2), w_pass_on(0)),
+        0: lambda: (w_begin(0, 1, (1, 3)), w_begin(1, 1, (1,)), own_heads()),
+        1: lambda: (w_begin(0, 1, (2,)), w_begin(1, 1, (3,))),
+        2: lambda: (w_begin(1, 1, (2,)), ring_pass_on(0, 0), ring_pass_on(1, 0), w_begin(2, 0), w_begin(3, 0)),
+        3: lambda: slab_arrived(0, 1, 3),
+        4: lambda: (slab_arrived(0, 2), slab_arrived(1, 1)),
+        5: lambda: (slab_arrived(1, 3), w_arrived(2, 0), w_begin(2, 1), w_arrived(3, 0), w_begin(3, 1)),
+        6: lambda: slab_arrived(1, 2),
+        7: lambda: [ring_pass_on(0, u) for u in (1, 3, 2)],
+        8: lambda: (w_arrived(2, 1), w_begin(2, 2), w_arrived(3, 1), w_begin(3, 2)),
+        11: lambda: (ring_pass_on(1, 1), w_arrived(3, 2), w_pass_on(3)),
     }
 
     @pl.loop(0, STEPS)
@@ -290,6 +344,10 @@
         @pl.when(n + 2 < STEPS)
         def _():
             relay_to_mate(n + 2)
+
+        @pl.when(n + 4 < STEPS)
+        def _():
+            begin_chunk(n + 4)
 
         @pl.when(n + 1 < STEPS)
         def _():
@@ -312,12 +370,17 @@
             ob[j] = (acc[:, :HS] / acc[:, HS:]).astype(jnp.bfloat16)
             send_attended(j)
 
+    for u in (3, 2):
+        ring_pass_on(1, u)
     w_arrived(2, 2)
     w_pass_on(2)
-    w_arrived(3, 2)
-    w_pass_on(3)
-    w_arrived(1, 2)
-    w_pass_on(1)
+
+    for j in range(3):
+        settle(qb.at[0, pl.ds(0, 7 * T)], q_send.at[j])
+        settle(kvb.at[0, pl.ds(0, 7)], kv_send.at[j])
+    settle(kvb.at[0, pl.ds(0, 3)], own_send)
+    settle(kvb.at[0, pl.ds(0, 21)], mate_send)
+    settle(kvb.at[:, pl.ds(0, 16)], part_send)
 
     for j in range(3):
         part = ob.at[j]
@@ -326,11 +389,11 @@
     def sum_copy(g, zb):
         first, count, _ = GROUPS[g]
         cols = pl.ds(pl.multiple_of(zb * 768 + first, HS), count)
-        return remote(theirs.at[:, cols], landed.at[:, cols], sum_send.at[g, zb], sum_recv.at[g, zb], partner)
-
-    order = (2, 3, 0, 1)
+        return remote(theirs.at[:, cols], landed.at[:, cols], sum_send, sum_recv.at[g, zb], partner)
+
+    order = (3, 0, 2, 1)
     for g in order:
-        w_complete(g)
+        (ring_complete if g < RINGS else w_complete)(g)
         first, count, _ = GROUPS[g]
 
         @pl.loop(0, 4)
@@ -341,13 +404,10 @@
                 total += jnp.dot(
                     ox[:, xb * 384 : (xb + 1) * 384], wb[xb, zb, :, first : first + count], preferred_element_type=jnp.float32
                 )
-            low, high = total[:T], total[T:]
-            mine[:, cols] = jnp.where(c == 0, low, high)
-            theirs[:, cols] = jnp.where(c == 0, high, low)
+            mine[:, cols] = total[:T]
+            theirs[:, cols] = total[T:]
             sum_copy(g, zb).start()
 
-    token = (s * 4 + z) * T + lax.broadcasted_iota(jnp.int32, (T, 1), 0)
-    live = token < len_ref[0]
     for g in order:
         first, count, _ = GROUPS[g]
 
@@ -355,49 +415,16 @@
         def _(zb, first=first, count=count, g=g):
             cols = pl.ds(pl.multiple_of(zb * 768 + first, HS), count)
             sum_copy(g, zb).wait_recv()
-            out_vm[:, cols] = jnp.where(live, mine[:, cols] + landed[:, cols], 0.0).astype(jnp.bfloat16)
+            out_vm[:, cols] = (mine[:, cols] + landed[:, cols]).astype(jnp.bfloat16)
 
     done = pltpu.make_async_copy(out_vm, out_hbm.at[0], out_sem)
     done.start()
 
-    @pl.loop(0, 3)
-    def _(j):
-        for which in range(2):
-            own_to_mate(j, which).wait_send()
-
-        @pl.loop(0, 4)
-        def _(dx):
-            for cross in range(2):
-                moves = [q_move(j, dx, cross), kv_move(j, dx, cross, 0), kv_move(j, dx, cross, 1)]
-                o = o_move(j, dx, cross)
-
-                def drain(moves=moves):
-                    for move in moves:
-                        remote(*move).wait_send()
-
-                def drain_o(o=o):
-                    remote(*o).wait_send()
-
-                if cross == 1:
-                    drain()
-                    drain_o()
-                else:
-                    pl.when(dx != 0)(drain)
-                    pl.when((dx != 0) | (p != c))(drain_o)
-
-    @pl.loop(0, STEPS)
-    def _(n):
-        pl.when(n % 4 == 0)(lambda: cross_copy(n).wait_send())
-        pl.when(n % 4 != 0)(lambda: mate_copy(n).wait_send())
-        part_copy(n).wait_send()
-
+    pl.when(p == c)(lambda: settle(ob.at[:, pl.ds(0, 7 * T)], o_send))
+    pl.when(p != c)(lambda: settle(ob, o_send))
     for g in range(len(GROUPS)):
         w_drain(g)
-
-        @pl.loop(0, 4)
-        def _(zb, g=g):
-            sum_copy(g, zb).wait_send()
-
+    settle(landed, sum_send)
     done.wait()
 
 
@@ -424,8 +451,8 @@
             vmem((T, D), f32),
             vmem((T, D), f32),
             vmem((T, D), bf16),
-            dma((3, 8)), dma((3, 8, 2)), dma((STEPS,)), dma((3, 2)), dma((STEPS,)), dma((3, 8)), dma((groups, 10)), dma((groups, 4)),
-            dma((3,)), dma((3, 4)), dma((STEPS,)), dma((STEPS,)), dma((3,)), dma((groups, 10)), dma((groups, 4)), dma(()), dma(()),
+            dma((3,)), dma((3,)), dma(()), dma(()), dma(()), dma(()), dma((groups, 4)), dma(()),
+            dma((3,)), dma((3, 4)), dma((STEPS,)), dma((STEPS,)), dma((3,)), dma((groups, 8)), dma((RINGS, 4, 4)), dma((groups, 4)), dma(()), dma(()),
         ],
         compiler_params=pltpu.CompilerParams(vmem_limit_bytes=60 * 2**20, has_side_effects=True, collective_id=0),
         cost_estimate=pl.CostEstimate(flops=16 * 10**9, bytes_accessed=30 * 2**20, transcendentals=0),
@@ -434,7 +461,10 @@
 
 
 def shards(queries, keys, values, lengths, out_weight):
-    return everything(lengths, queries, keys, values, out_weight)
+    s, z = lax.axis_index("seq"), lax.axis_index("tensor")
+    token = (s * 4 + z) * T + jnp.arange(T, dtype=jnp.int32)
+    projected = everything(lengths, queries, keys, values, out_weight)
+    return jnp.where((token < lengths[0])[None, :, None], projected, jnp.bfloat16(0))
 
 
 def solution(mesh):

time: 134 us -> 104 us (0.78)
  Pallas kernels: 131 us -> 101 us
  other arithmetic: 0 us -> 2.14 us
  local copies, waits for them, and re-layouts: 2.06 us -> 0 us
    pallas_call x1, Pallas kernels: 131 us -> 101 us  [everything(): pl.pallas_call(kernel, out_shape=jax.ShapeDtypeStruct((1, T, D), bf16), i...]
    select_n x0 -> x1, other arithmetic: none -> 2.14 us  [shards(): jnp.where((token < lengths[0])[None, :, None], projected, jnp.bfloat16(0))]
    unnamed x1 -> x0, local copies, waits for them, and re-layouts: 2.06 us -> none
where the time goes in v3:
time: 104 us; the launch traced here: 103 us
  Pallas kernels  101 us (97%)
  other arithmetic  2.14 us (2%)
    pallas_call x1, Pallas kernels, everything(): pl.pallas_call(kernel, out_shape=jax.ShapeDtypeStruct((1, T, D), bf16), i...  101 us
    select_n x1, other arithmetic, shards(): jnp.where((token < lengths[0])[None, :, None], projected, jnp.bfloat16(0))  2.14 us

profile of v3, /device:TPU:1, one launch (start us, length us, event | category | flops | bytes accessed | tf_op | source)
XLA Modules:
  0.0 103.4 jit_solution(18292782925002622164)
XLA Ops:
  0.7 100.6 %attend.1 = bf16[1,128,3072]{2,1,0:T(8,128)(2,1)} custom-call(s32[1]{0:T(128)} %copy.6.len_ref, bf16[1,128,3072]{2,1,0:T(8,128)(2,1)} %q_hbm.1, bf16[1,128,3072]{2,1,0:T(8,128)(2,1)} %k_hbm.1, bf16[1,128,3072]{2,1,0:T(8,128)(2,1)} %v_hbm.1, bf16[96,768]{1,0:T(8,128)(2,1)} %w_hbm.1), custom_call_target="tpu_custom_call" | custom-call | flops 16000000000 | bytes 31457280 | tf_op jit(solution)/shard_map/attend/pallas_call | solution.py:436
  101.3 2.1 %broadcast_select_fusion = bf16[1,128,3072]{2,1,0:T(8,128)(2,1)} fusion(bf16[1,128,3072]{2,1,0:T(8,128)(2,1)} %attend.1, pred[128]{0:T(512)(128)(4,1)S(1)} %add_compare_fusion), kind=kLoop, calls=%fused_computation | loop fusion | flops 393216 | bytes 1572992 | tf_op jit(solution)/shard_map/jit(_where)/select_n | solution.py:467
  (1 shorter events, 0.0 us)
